TPU v7x, 32 devices: a whole 2x2x4 slice. The times are simulated.
32 devices in a mesh: seq: 4 (over z), tp: 4 (over y, x), dp: 2 (over core).
Axes of the slice: x: 2, y: 2, z: 4, core: 2. Of those that a mesh axis runs over, the one named last changes fastest.
Arguments:
- x_ckpt: bfloat16 [1024, 5120], P(('dp', 'seq', 'tp')), parts along dimension 0, may hold values from -5 to 5
- bc_ckpt: bfloat16 [2, 1024, 128], P(None, ('dp', 'seq', 'tp')), parts along dimension 1, may hold values from -1 to 1
- step_sizes: float32 [80, 1024], P('tp', ('dp', 'seq')), parts along dimension 1, may hold values from 0.03 to 0.3
- decay_rate: float32 [80], P('tp'), may hold values from 0 to 1, as said below
- skip_gain: float32 [80], P('tp'), may hold values from 0.25 to 1.75
- grad_out: bfloat16 [1024, 5120], P(('dp', 'seq'), 'tp'), parts along dimension 0, may hold values from -3 to 3
Outputs:
- grad_x: bfloat16 [1024, 5120], P(('dp', 'seq'), 'tp'), parts along dimension 0
- grad_bc: float32 [2, 1024, 128], P(None, ('dp', 'seq', 'tp')), parts along dimension 1
- grad_step: float32 [80, 1024], P('tp', ('dp', 'seq')), parts along dimension 1
There are 2 independent parts, one for each index of `dp`. A program takes and returns all parts, laid end to end along the dimension named above; an argument that names none is the same for every part. Nothing has to cross between parts.
Inputs may be any that keep to these rules, and one draw needn't show every extreme that they name: `decay_rate`: positive decay rates of the 80 heads.
All inputs are finite; a program needn't handle non-finite values.
Results may differ from a plain program's by a relative error of at most 0.001.
Values may be sent and summed in bfloat16 or wider, within the bound.
No kernel may reach another device: no remote copies, remote signals or barrier semaphores. Data moves between devices by JAX's collectives and lax.ppermute only.
A program may use at most 128 MiB of HBM per device.

v0:
```python
from functools import partial
import jax
import jax.numpy as jnp
from jax import lax
from jax.sharding import PartitionSpec as P

BLOCK = 128
highest = lax.Precision.HIGHEST


def carried_in(array, axis, combine, identity, reverse):
    peers, index = (lax.axis_size(axis), lax.axis_index(axis))
    everything = jax.tree.map(lambda part: lax.all_gather(part, axis), array)
    start = jax.tree.map(
        lambda part, zero: jnp.broadcast_to(jnp.asarray(zero, part.dtype), part.shape),
        array,
        identity,
    )

    def hop(k, before):
        at = peers - 1 - k if reverse else k
        reached = at > index if reverse else at < index
        new = combine(before, jax.tree.map(lambda part: part[at], everything))
        return jax.tree.map(lambda a, b: jnp.where(reached, a, b), new, before)

    return lax.fori_loop(0, peers, hop, start)


def block_step(head_rates, head_gains, carry_state, pieces):
    inputs, step_block, proj_b, proj_c = pieces
    head_count = step_block.shape[0]
    row_count = step_block.shape[1]
    values = inputs.astype(jnp.float32).reshape(row_count, head_count, -1)
    cumulative = jnp.cumsum(-head_rates[:, None] * step_block, axis=1)
    positions = jnp.arange(row_count, dtype=jnp.int32)
    causal = positions[:, None] >= positions[None, :]
    log_gaps = cumulative[:, :, None] - cumulative[:, None, :]
    within = jnp.where(causal, jnp.exp(jnp.where(causal, log_gaps, 0.0)), 0.0)
    scores = jnp.dot(proj_c, proj_b.T, precision=highest, preferred_element_type=jnp.float32)
    weights = within * scores[None, :, :] * step_block[:, None, :]
    local_part = jnp.einsum(
        "hts,shp->thp", weights, values, precision=highest, preferred_element_type=jnp.float32
    )
    carried = jnp.einsum(
        "tn,hpn->thp", proj_c, carry_state, precision=highest, preferred_element_type=jnp.float32
    )
    carried = carried * jnp.exp(cumulative).T[:, :, None]
    result = local_part + carried + head_gains[None, :, None] * values
    tail_weight = jnp.exp(cumulative[:, -1:] - cumulative) * step_block
    fresh_state = jnp.einsum(
        "hs,shp,sn->hpn",
        tail_weight,
        values,
        proj_b,
        precision=highest,
        preferred_element_type=jnp.float32,
    )
    final_state = jnp.exp(cumulative[:, -1])[:, None, None] * carry_state + fresh_state
    return (final_state, result.reshape(row_count, -1))


def run_blocks(inputs, step_sizes, proj_b, proj_c, start_state, head_rates, head_gains, block_rows):
    row_count = inputs.shape[0]
    block_count = row_count // block_rows
    head_count = step_sizes.shape[0]
    input_blocks = inputs.reshape(block_count, block_rows, inputs.shape[1])
    step_blocks = step_sizes.reshape(head_count, block_count, block_rows).transpose(1, 0, 2)
    b_blocks = proj_b.reshape(block_count, block_rows, proj_b.shape[1])
    c_blocks = proj_c.reshape(block_count, block_rows, proj_c.shape[1])
    stepper = jax.checkpoint(partial(block_step, head_rates, head_gains))
    final_state, results = lax.scan(
        stepper, start_state, (input_blocks, step_blocks, b_blocks, c_blocks)
    )
    return (results.reshape(row_count, -1), final_state)


def combine(earlier, later):
    return (earlier[0] * later[0], later[0][:, None, None] * earlier[1] + later[1])


def shards(x_ckpt, bc_ckpt, step_sizes, decay_rate, skip_gain, grad_out):
    head_count = decay_rate.shape[0]
    width = grad_out.shape[1]
    own_rows = lax.all_to_all(x_ckpt, "tp", split_axis=1, concat_axis=0, tiled=True)
    pairs = lax.all_gather(bc_ckpt, "tp", axis=1, tiled=True)
    proj_b = pairs[0].astype(jnp.float32)
    proj_c = pairs[1].astype(jnp.float32)
    token_count = own_rows.shape[0]
    head_width = width // head_count
    values = own_rows.astype(jnp.float32).reshape(token_count, head_count, head_width)
    cumulative = jnp.cumsum(-decay_rate[:, None] * step_sizes, axis=1)
    passing = jnp.exp(cumulative[:, -1])
    tail_weight = jnp.exp(cumulative[:, -1:] - cumulative) * step_sizes
    summary = jnp.einsum(
        "hs,shp,sn->hpn",
        tail_weight,
        values,
        proj_b,
        precision=highest,
        preferred_element_type=jnp.float32,
    )
    upstream = grad_out.astype(jnp.float32)
    pulled = jnp.einsum(
        "ht,thp,tn->hpn",
        jnp.exp(cumulative),
        upstream.reshape(token_count, head_count, head_width),
        proj_c,
        precision=highest,
        preferred_element_type=jnp.float32,
    )
    neutral = (jnp.ones_like(passing), jnp.zeros_like(summary))
    entering = carried_in((passing, summary), "seq", combine, neutral, False)[1]
    leaving = carried_in((passing, pulled), "seq", combine, neutral, True)[1]

    def forward(inputs, basis_b, basis_c, step_block, start_state):
        return run_blocks(
            inputs, step_block, basis_b, basis_c, start_state, decay_rate, skip_gain, BLOCK
        )

    outputs, pull_back = jax.vjp(forward, own_rows, proj_b, proj_c, step_sizes, entering)
    grad_x, grad_b, grad_c, grad_step, unused = pull_back((upstream, leaving))
    partial_grads = jnp.stack([grad_b, grad_c])
    grad_bc = lax.psum_scatter(partial_grads, "tp", scatter_dimension=1, tiled=True)
    return (grad_x, grad_bc, grad_step)


def solution(mesh):
    return jax.shard_map(
        shards,
        mesh=mesh,
        in_specs=(
            P(("dp", "seq", "tp"), None),
            P(None, ("dp", "seq", "tp"), None),
            P("tp", ("dp", "seq")),
            P("tp"),
            P("tp"),
            P(("dp", "seq"), "tp"),
        ),
        out_specs=(
            P(("dp", "seq"), "tp"),
            P(None, ("dp", "seq", "tp"), None),
            P("tp", ("dp", "seq")),
        ),
        check_vma=False,
    )
```

profile of v0, /device:TPU:0, one launch (start us, length us, event | category | flops | bytes accessed | tf_op | source)
XLA Modules:
  0.0 178.6 jit_solution(7967003669195045583)
XLA Ops:
  7.2 0.0 all-gather.8.cloned.1.call-start
  7.2 0.7 neg.18
  7.9 0.8 broadcast_multiply_fusion.2
  8.6 0.3 reduce_window_sum.34
  8.9 0.2 slice_reduce_fusion.1
  9.1 0.8 exponential_bitcast_fusion
  9.9 9.9 %all_gather.22 = bf16[2,128,128]{2,1,0:T(8,128)(2,1)S(1)} all-gather(bf16[2,32,128]{2,1,0:T(8,128)(2,1)} %param.11), channel_id=1, replica_groups=mesh['seq'=4,'tp'=4,'dp'=2] {'tp'}, dimensions={1}, use_global_device_ids=true | all-gather | bytes 81920 | tf_op jit(solution)/shard_map/all_gather | solution.py:85
  19.8 1.2 copy.35
  21.1 1.3 fusion.32
  22.3 0.0 all-gather.8.cloned.1.call-update
  22.4 0.7 copy.53
  23.1 3.5 %all-to-all-start = ((bf16[32,4,1280]{2,0,1:T(8,128)(2,1)}), bf16[32,4,1280]{2,0,1:T(8,128)(2,1)S(1)}, u32[]{:S(2)}, u32[]{:S(2)}) async-start(bf16[32,4,1280]{2,0,1:T(8,128)(2,1)} %bitcast.97), calls=%async_computation | async-start | bytes 655360 | tf_op jit(solution)/shard_map/all_to_all | solution.py:84
  26.6 0.0 all-gather.6.cloned.1.call-start
  26.6 0.1 copy.32
  26.7 5.4 %all-to-all-done = bf16[32,4,1280]{2,0,1:T(8,128)(2,1)S(1)} async-done(((bf16[32,4,1280]{2,0,1:T(8,128)(2,1)}), bf16[32,4,1280]{2,0,1:T(8,128)(2,1)S(1)}, u32[]{:S(2)}, u32[]{:S(2)}) %all-to-all-start) | async-done | bytes 327712 | tf_op jit(solution)/shard_map/all_to_all | solution.py:84
  32.2 0.4 reshape.105
  32.6 0.2 copy-done
  32.8 0.5 broadcast_multiply_fusion
  33.3 0.0 copy-start.7
  33.3 2.0 %fusion.2 = f32[20,64,128]{2,1,0:T(8,128)} fusion(f32[128,20,64]{2,1,0:T(8,128)S(1)} %broadcast_multiply_fusion, bf16[2,128,128]{2,1,0:T(8,128)(2,1)S(1)} %all_gather.22), kind=kOutput, calls=%fused_computation.6 | convolution fusion | flops 251658240 | bytes 2260992 | tf_op jit(solution)/shard_map/hs,shp,sn->hpn/dot_general | solution.py:94
  35.4 0.0 all-gather.6.cloned.1.call-update
  35.4 0.0 reduce-scatter.2.cloned.1.call-start
  35.5 0.6 dynamic-slice.5
  36.7 0.2 dynamic-update-slice
  37.0 12.7 %all-reduce.2 = f32[80]{0:T(128)S(1)} all-reduce(f32[80]{0:T(128)S(1)} %dynamic-update-slice), channel_id=2, replica_groups=mesh['seq'=4,'tp'=4,'dp'=2] {'seq'}, use_global_device_ids=true, to_apply=%add.2 | all-reduce | flops 80 | bytes 640
  49.7 0.1 reshape.107
  49.8 0.8 bitcast_convert_fusion.1
  50.6 27.2 %all-gather.8.cloned.1.call-done = f32[80,64,128]{2,1,0:T(8,128)} async-done(((f32[20,64,128]{2,1,0:T(8,128)}), f32[80,64,128]{2,1,0:T(8,128)}) %all-gather.8.cloned.1.call-update) | async-done | bytes 2621456 | tf_op jit(solution)/shard_map/all_gather | solution.py:13
  77.7 5.1 %while.21 = (s32[]{:T(128)}, f32[20,64,128]{2,1,0:T(8,128)S(1)}, s32[]{:T(128)}, f32[4,20]{1,0:T(4,128)S(1)}, f32[4,20,64,128]{3,2,1,0:T(8,128)}, /*index=5*/s32[]{:T(128)}, s32[]{:T(128)}, s32[]{:T(128)}, s32[]{:T(128)}) while((s32[]{:T(128)}, f32[20,64,128]{2,1,0:T(8,128)S(1)}, s32[]{:T(128)}, f32[4,20]{1,0:T(4,128)S(1)}, ...), condition=%wide.region_4.5_spmd.clone, body=%wide.region_3.4_spmd.clone.sunk | while | flops 655368 | bytes 1966487 | solution.py:26
  77.8 1.2 fusion.67
  79.0 1.2 fusion.67
  80.3 1.2 fusion.67
  81.6 1.2 fusion.67
  82.8 50.0 %all-gather.6.cloned.1.call-done = f32[80,64,128]{2,1,0:T(8,128)} async-done(((f32[20,64,128]{2,1,0:T(8,128)}), f32[80,64,128]{2,1,0:T(8,128)}) %all-gather.6.cloned.1.call-update) | async-done | bytes 2621456 | tf_op jit(solution)/shard_map/all_gather | solution.py:13
  132.8 5.1 %while.20 = (s32[]{:T(128)}, f32[20,64,128]{2,1,0:T(8,128)S(1)}, s32[]{:T(128)}, f32[4,20]{1,0:T(4,128)S(1)}, f32[4,20,64,128]{3,2,1,0:T(8,128)}, /*index=5*/s32[]{:T(128)}, s32[]{:T(128)}) while((s32[]{:T(128)}, f32[20,64,128]{2,1,0:T(8,128)S(1)}, s32[]{:T(128)}, f32[4,20]{1,0:T(4,128)S(1)}, f32[4,20,64,128]{3,2,1,0:T(8,128)}, ...), condition=%wide.region_2.3_spmd.clone, body=%wide.region_1.2_spmd.clone.sunk | while | flops 655364 | bytes 1966425 | solution.py:26
  132.8 1.2 fusion.66
  134.1 1.2 fusion.66
  135.4 1.2 fusion.66
  136.7 1.2 fusion.66
  137.9 0.1 broadcast_multiply_fusion.1
  138.0 0.3 reduce_window_sum.35
  138.3 0.2 multiply_reduce_fusion.2
  138.5 0.1 copy.37
  138.6 0.2 copy-done.1
  138.9 0.2 copy.36
  139.1 0.2 exponential_multiply_fusion
  139.3 0.7 fusion.23
  140.0 0.2 fusion.48
  140.2 0.1 copy.38
  140.3 0.3 fusion.50
  140.5 0.7 fusion.18
  141.2 2.2 %fusion.22 = (f32[20,128]{1,0:T(8,128)S(1)}, f32[20,128]{1,0:T(8,128)S(1)}, f32[20,128]{1,0:T(8,128)S(1)}, f32[128,128]{1,0:T(8,128)S(1)}) fusion(f32[20,128]{1,0:T(8,128)S(1)} %copy-done.4, f32[128,128]{1,0:T(8,128)S(1)} %fusion.50, f32[20,128]{1,0:T(8,128)S(1)} %reduce_window_sum.35, pred[128,128]{1,0:T(8,128)(4,1)S(1)} %iota_compare_fusion, ...), kind=kOutput, calls=%fused_computation.29 | convolution fusion | flops 256549376 | bytes 1181696 | tf_op jit(solution)/shard_map/transpose(jvp())/while/body/eval_jaxpr/checkpoint/hts,shp->thp/dot_general | solution.py:41
  143.4 0.1 fusion.47
  143.5 1.2 convolution_bitcast_fusion.1
  144.7 1.2 reduce_window_sum.36
  146.0 0.7 multiply_add_fusion
  146.6 1.2 convolution_bitcast_fusion
  147.9 0.3 fusion.20
  148.2 0.2 fusion.19
  148.4 0.6 pad_maximum_fusion
  149.0 0.0 reduce-scatter.2.cloned.1.call-update
  149.0 1.6 fusion.15
  150.7 0.9 copy.39
  151.6 20.5 %reduce-scatter.2.cloned.1.call-done = f32[2,32,128]{2,1,0:T(8,128)} async-done(((f32[2,128,128]{2,1,0:T(8,128)}), f32[2,32,128]{2,1,0:T(8,128)}) %reduce-scatter.2.cloned.1.call-update) | async-done | bytes 32784 | tf_op jit(solution)/shard_map/reduce_scatter | solution.py:123
  (28 shorter events, 0.2 us)
Async XLA Ops:
  7.2 70.6 %all-gather.8.cloned.1.call-start = ((), (), s32[]{:S(2)}) async-start(), calls=%async_computation.4 | async-start | bytes 3276800 | tf_op jit(solution)/shard_map/all_gather | solution.py:13
  19.8 13.5 %copy-start.2 = (bf16[2,128,128]{2,1,0:T(8,128)(2,1)}, bf16[2,128,128]{2,1,0:T(8,128)(2,1)S(1)}, u32[]{:S(2)}) copy-start(bf16[2,128,128]{2,1,0:T(8,128)(2,1)S(1)} %all_gather.22) | copy-start | bytes 196612
  21.0 1.4 copy-start.3
  23.1 9.0 %all-to-all-start = ((bf16[32,4,1280]{2,0,1:T(8,128)(2,1)}), bf16[32,4,1280]{2,0,1:T(8,128)(2,1)S(1)}, u32[]{:S(2)}, u32[]{:S(2)}) async-start(bf16[32,4,1280]{2,0,1:T(8,128)(2,1)} %bitcast.97), calls=%async_computation | async-start | bytes 655360 | tf_op jit(solution)/shard_map/all_to_all | solution.py:84
  26.6 106.2 %all-gather.6.cloned.1.call-start = ((), (), s32[]{:S(2)}) async-start(), calls=%async_computation.3 | async-start | bytes 3276800 | tf_op jit(solution)/shard_map/all_gather | solution.py:13
  32.1 0.7 copy-start
  33.3 2.2 %copy-start.7 = (u32[32]{0:T(128)S(1)}, u32[32]{0:T(128)}, u32[]{:S(2)}) copy-start(u32[32]{0:T(128)} %constant.131) | copy-start | bytes 388
  35.4 136.7 %reduce-scatter.2.cloned.1.call-start = ((), (), s32[]{:S(2)}) async-start(), calls=%async_computation.2 | async-start | bytes 163840 | tf_op jit(solution)/shard_map/reduce_scatter | solution.py:123
  132.8 5.1 %copy-start.5 = (f32[20]{0:T(128)S(1)}, f32[20]{0:T(128)}, u32[]{:S(2)}) copy-start(f32[20]{0:T(128)} %param.13) | copy-start | bytes 244
  132.8 5.1 %copy-start.4 = (f32[20,128]{1,0:T(8,128)S(1)}, f32[20,128]{1,0:T(8,128)}, u32[]{:S(2)}) copy-start(f32[20,128]{1,0:T(8,128)} %param.12) | copy-start | bytes 30724
  137.9 1.0 copy-start.1
  144.7 4.3 %copy-start.6 = (f32[20]{0:T(128)S(1)}, f32[20]{0:T(128)}, u32[]{:S(2)}) copy-start(f32[20]{0:T(128)} %param.14) | copy-start | bytes 244
Sparse Core Ops, SparseCore 0:
  22.5 55.2 all-gather.7
  79.3 53.4 all-gather.5
  149.2 22.8 reduce-scatter.1
where the time goes:
time: 179 us
  waiting for transfers between devices  103 us (58%)
  blocking collectives  22.6 us (13%)
  other arithmetic  17.4 us (10%)
  between operations  14.6 us (8%)
  matrix products  11.7 us (7%)
  local copies, waits for them, and re-layouts  5.46 us (3%)
  starting transfers between devices  3.58 us (2%)
    all_gather x2, waiting for transfers between devices, carried_in(): everything = jax.tree.map(lambda part: lax.all_gather(part, axis), array)  77.2 us
    reduce_scatter x1, waiting for transfers between devices, shards(): lax.psum_scatter(partial_grads, 'tp', scatter_dimension=1, tiled=True)  20.5 us
    unnamed x1, blocking collectives  12.7 us
    all_gather x1, blocking collectives, shards(): pairs = lax.all_gather(bc_ckpt, 'tp', axis=1, tiled=True)  9.88 us
    select_n x8, other arithmetic, hop(): return jax.tree.map(lambda a, b: jnp.where(reached, a, b), new, before)  9.87 us
    all_to_all x1, waiting for transfers between devices, shards(): lax.all_to_all(x_ckpt, 'tp', split_axis=1, concat_axis=0, tiled=True)  5.35 us
    dot_general x2, matrix products, block_step(): jnp.einsum('hts,shp->thp', weights, values, precision=highest, preferred_...  3.77 us
  transfers between devices with their start and end apart: 4, of which 4 were waited for; matrix products, arithmetic and copies ran while one was open for 7% of the time, Pallas kernels for 0%

commit v1 on v0

--- a/solution.py
+++ b/solution.py
@@ -3,6 +3,7 @@
 import jax.numpy as jnp
 from jax import lax
 from jax.sharding import PartitionSpec as P
+from jax.lax import all_to_all, axis_size
 
 BLOCK = 128
 highest = lax.Precision.HIGHEST
@@ -81,7 +82,16 @@
 def shards(x_ckpt, bc_ckpt, step_sizes, decay_rate, skip_gain, grad_out):
     head_count = decay_rate.shape[0]
     width = grad_out.shape[1]
-    own_rows = lax.all_to_all(x_ckpt, "tp", split_axis=1, concat_axis=0, tiled=True)
+
+    def launch_cube_on_mesh(net_axis, x_part):
+        opened = axis_size(net_axis)
+        current_value = jnp.split(x_part, opened, 1)
+        value_now = jnp.stack(current_value, 0)
+        w2 = all_to_all(value_now, axis_name=net_axis, split_axis=0, concat_axis=0)
+        parts_out = jnp.concatenate(w2, 0)
+        return parts_out
+
+    own_rows = launch_cube_on_mesh("tp", x_ckpt)
     pairs = lax.all_gather(bc_ckpt, "tp", axis=1, tiled=True)
     proj_b = pairs[0].astype(jnp.float32)
     proj_c = pairs[1].astype(jnp.float32)

time: 179 us -> 180 us (level)
  no operation moved by 1% of the time
where the time goes in v1:
time: 180 us; the launch traced here: 179 us
  waiting for transfers between devices  103 us (57%)
  blocking collectives  22.6 us (13%)
  other arithmetic  18.1 us (10%)
  between operations  14.6 us (8%)
  matrix products  11.7 us (6%)
  local copies, waits for them, and re-layouts  4.64 us (3%)
  starting transfers between devices  3.58 us (2%)
    all_gather x2, waiting for transfers between devices, carried_in(): everything = jax.tree.map(lambda part: lax.all_gather(part, axis), array)  77.3 us
    reduce_scatter x1, waiting for transfers between devices, shards(): lax.psum_scatter(partial_grads, 'tp', scatter_dimension=1, tiled=True)  20.5 us
    unnamed x1, blocking collectives  12.7 us
    all_gather x1, blocking collectives, shards(): pairs = lax.all_gather(bc_ckpt, 'tp', axis=1, tiled=True)  9.88 us
    select_n x8, other arithmetic, hop(): return jax.tree.map(lambda a, b: jnp.where(reached, a, b), new, before)  9.86 us
    all_to_all x1, waiting for transfers between devices, launch_cube_on_mesh(): w2 = all_to_all(value_now, axis_name=net_axis, split_axis=0, concat_axis=0)  5.35 us
    dot_general x2, matrix products, block_step(): jnp.einsum('hts,shp->thp', weights, values, precision=highest, preferred_...  3.74 us
  transfers between devices with their start and end apart: 4, of which 4 were waited for; matrix products, arithmetic and copies ran while one was open for 7% of the time, Pallas kernels for 0%

profile of v1, /device:TPU:0, one launch (start us, length us, event | category | flops | bytes accessed | tf_op | source)
XLA Modules:
  0.0 178.7 jit_solution(18374866715695577578)
XLA Ops:
  7.2 0.0 all-gather.8.cloned.1.call-start
  7.2 0.7 neg.18
  7.9 0.8 broadcast_multiply_fusion.2
  8.6 0.3 reduce_window_sum.34
  8.9 0.2 slice_reduce_fusion.1
  9.1 0.8 exponential_bitcast_fusion
  9.9 9.9 %all_gather.22 = bf16[2,128,128]{2,1,0:T(8,128)(2,1)S(1)} all-gather(bf16[2,32,128]{2,1,0:T(8,128)(2,1)} %param.11), channel_id=1, replica_groups=mesh['seq'=4,'tp'=4,'dp'=2] {'tp'}, dimensions={1}, use_global_device_ids=true | all-gather | bytes 81920 | tf_op jit(solution)/shard_map/all_gather | solution.py:95
  19.8 1.2 copy.25
  21.1 1.3 fusion.32
  22.3 0.0 all-gather.8.cloned.1.call-update
  22.4 0.8 pad_maximum_fusion
  23.2 3.5 %all-to-all-start = ((bf16[4,32,1280]{2,1,0:T(8,128)(2,1)}), bf16[4,32,1280]{2,1,0:T(8,128)(2,1)S(1)}, u32[]{:S(2)}, u32[]{:S(2)}) async-start(bf16[4,32,1280]{2,1,0:T(8,128)(2,1)} %pad_maximum_fusion), calls=%async_computation | async-start | bytes 655360 | tf_op jit(solution)/shard_map/all_to_all | solution.py:90
  26.6 0.0 all-gather.6.cloned.1.call-start
  26.7 0.1 copy.23
  26.8 5.4 %all-to-all-done = bf16[4,32,1280]{2,1,0:T(8,128)(2,1)S(1)} async-done(((bf16[4,32,1280]{2,1,0:T(8,128)(2,1)}), bf16[4,32,1280]{2,1,0:T(8,128)(2,1)S(1)}, u32[]{:S(2)}, u32[]{:S(2)}) %all-to-all-start) | async-done | bytes 327712 | tf_op jit(solution)/shard_map/all_to_all | solution.py:90
  32.2 0.4 reshape.101
  32.6 0.5 broadcast_multiply_fusion
  33.1 0.0 copy-start.7
  33.1 2.0 %fusion.2 = f32[20,64,128]{2,1,0:T(8,128)} fusion(f32[128,20,64]{2,1,0:T(8,128)S(1)} %broadcast_multiply_fusion, bf16[2,128,128]{2,1,0:T(8,128)(2,1)S(1)} %all_gather.22), kind=kOutput, calls=%fused_computation.6 | convolution fusion | flops 251658240 | bytes 2260992 | tf_op jit(solution)/shard_map/hs,shp,sn->hpn/dot_general | solution.py:104
  35.2 0.0 all-gather.6.cloned.1.call-update
  35.2 0.0 reduce-scatter.2.cloned.1.call-start
  35.3 0.6 dynamic-slice.5
  36.5 0.2 dynamic-update-slice
  36.8 12.7 %all-reduce.2 = f32[80]{0:T(128)S(1)} all-reduce(f32[80]{0:T(128)S(1)} %dynamic-update-slice), channel_id=2, replica_groups=mesh['seq'=4,'tp'=4,'dp'=2] {'seq'}, use_global_device_ids=true, to_apply=%add.2 | all-reduce | flops 80 | bytes 640
  49.5 0.1 reshape.103
  49.6 0.8 bitcast_convert_fusion
  50.4 27.4 %all-gather.8.cloned.1.call-done = f32[80,64,128]{2,1,0:T(8,128)} async-done(((f32[20,64,128]{2,1,0:T(8,128)}), f32[80,64,128]{2,1,0:T(8,128)}) %all-gather.8.cloned.1.call-update) | async-done | bytes 2621456 | tf_op jit(solution)/shard_map/all_gather | solution.py:14
  77.8 5.1 %while.21 = (s32[]{:T(128)}, f32[20,64,128]{2,1,0:T(8,128)S(1)}, s32[]{:T(128)}, f32[4,20]{1,0:T(4,128)S(1)}, f32[4,20,64,128]{3,2,1,0:T(8,128)}, /*index=5*/s32[]{:T(128)}, s32[]{:T(128)}, s32[]{:T(128)}, s32[]{:T(128)}) while((s32[]{:T(128)}, f32[20,64,128]{2,1,0:T(8,128)S(1)}, s32[]{:T(128)}, f32[4,20]{1,0:T(4,128)S(1)}, ...), condition=%wide.region_4.5_spmd.clone, body=%wide.region_3.4_spmd.clone.sunk | while | flops 655368 | bytes 1966487 | solution.py:27
  77.8 1.2 fusion.67
  79.0 1.2 fusion.67
  80.3 1.2 fusion.67
  81.6 1.2 fusion.67
  82.9 50.0 %all-gather.6.cloned.1.call-done = f32[80,64,128]{2,1,0:T(8,128)} async-done(((f32[20,64,128]{2,1,0:T(8,128)}), f32[80,64,128]{2,1,0:T(8,128)}) %all-gather.6.cloned.1.call-update) | async-done | bytes 2621456 | tf_op jit(solution)/shard_map/all_gather | solution.py:14
  132.8 5.1 %while.20 = (s32[]{:T(128)}, f32[20,64,128]{2,1,0:T(8,128)S(1)}, s32[]{:T(128)}, f32[4,20]{1,0:T(4,128)S(1)}, f32[4,20,64,128]{3,2,1,0:T(8,128)}, /*index=5*/s32[]{:T(128)}, s32[]{:T(128)}) while((s32[]{:T(128)}, f32[20,64,128]{2,1,0:T(8,128)S(1)}, s32[]{:T(128)}, f32[4,20]{1,0:T(4,128)S(1)}, f32[4,20,64,128]{3,2,1,0:T(8,128)}, ...), condition=%wide.region_2.3_spmd.clone, body=%wide.region_1.2_spmd.clone.sunk | while | flops 655364 | bytes 1966425 | solution.py:27
  132.8 1.2 fusion.66
  134.1 1.2 fusion.66
  135.4 1.2 fusion.66
  136.6 1.2 fusion.66
  137.9 0.2 multiply_reduce_fusion.2
  138.2 0.1 copy.27
  138.3 0.3 copy-done.5
  138.5 0.1 copy-done.4
  138.6 0.1 broadcast_multiply_fusion.1
  138.7 0.3 reduce_window_sum.35
  139.0 0.2 copy.26
  139.2 0.2 exponential_multiply_fusion
  139.4 0.7 fusion.23
  140.1 0.2 fusion.48
  140.3 0.1 copy.28
  140.4 0.3 fusion.50
  140.6 0.7 fusion.18
  141.3 2.1 %fusion.22 = (f32[20,128]{1,0:T(8,128)S(1)}, f32[20,128]{1,0:T(8,128)S(1)}, f32[20,128]{1,0:T(8,128)S(1)}, f32[128,128]{1,0:T(8,128)S(1)}) fusion(f32[20,128]{1,0:T(8,128)S(1)} %copy-done.4, f32[128,128]{1,0:T(8,128)S(1)} %fusion.50, f32[20,128]{1,0:T(8,128)S(1)} %reduce_window_sum.35, pred[128,128]{1,0:T(8,128)(4,1)S(1)} %iota_compare_fusion, ...), kind=kOutput, calls=%fused_computation.29 | convolution fusion | flops 256549376 | bytes 1181696 | tf_op jit(solution)/shard_map/transpose(jvp())/while/body/eval_jaxpr/checkpoint/hts,shp->thp/dot_general | solution.py:42
  143.5 0.1 fusion.47
  143.6 1.2 convolution_bitcast_fusion.1
  144.8 1.2 reduce_window_sum.36
  146.0 0.7 multiply_add_fusion
  146.7 1.2 convolution_bitcast_fusion
  147.9 0.3 fusion.20
  148.2 0.2 fusion.19
  148.4 0.6 pad_maximum_fusion.1
  149.1 0.0 reduce-scatter.2.cloned.1.call-update
  149.1 1.6 fusion.15
  150.7 0.9 copy.29
  151.6 20.5 %reduce-scatter.2.cloned.1.call-done = f32[2,32,128]{2,1,0:T(8,128)} async-done(((f32[2,128,128]{2,1,0:T(8,128)}), f32[2,32,128]{2,1,0:T(8,128)}) %reduce-scatter.2.cloned.1.call-update) | async-done | bytes 32784 | tf_op jit(solution)/shard_map/reduce_scatter | solution.py:133
  (28 shorter events, 0.2 us)
Async XLA Ops:
  7.2 70.6 %all-gather.8.cloned.1.call-start = ((), (), s32[]{:S(2)}) async-start(), calls=%async_computation.4 | async-start | bytes 3276800 | tf_op jit(solution)/shard_map/all_gather | solution.py:14
  19.8 13.3 %copy-start.2 = (bf16[2,128,128]{2,1,0:T(8,128)(2,1)}, bf16[2,128,128]{2,1,0:T(8,128)(2,1)S(1)}, u32[]{:S(2)}) copy-start(bf16[2,128,128]{2,1,0:T(8,128)(2,1)S(1)} %all_gather.22) | copy-start | bytes 196612
  21.0 1.4 copy-start.3
  23.2 9.0 %all-to-all-start = ((bf16[4,32,1280]{2,1,0:T(8,128)(2,1)}), bf16[4,32,1280]{2,1,0:T(8,128)(2,1)S(1)}, u32[]{:S(2)}, u32[]{:S(2)}) async-start(bf16[4,32,1280]{2,1,0:T(8,128)(2,1)} %pad_maximum_fusion), calls=%async_computation | async-start | bytes 655360 | tf_op jit(solution)/shard_map/all_to_all | solution.py:90
  26.6 106.2 %all-gather.6.cloned.1.call-start = ((), (), s32[]{:S(2)}) async-start(), calls=%async_computation.3 | async-start | bytes 3276800 | tf_op jit(solution)/shard_map/all_gather | solution.py:14
  32.2 0.9 copy-start
  33.1 2.2 %copy-start.7 = (u32[32]{0:T(128)S(1)}, u32[32]{0:T(128)}, u32[]{:S(2)}) copy-start(u32[32]{0:T(128)} %constant.131) | copy-start | bytes 388
  35.2 137.0 %reduce-scatter.2.cloned.1.call-start = ((), (), s32[]{:S(2)}) async-start(), calls=%async_computation.2 | async-start | bytes 163840 | tf_op jit(solution)/shard_map/reduce_scatter | solution.py:133
  137.9 0.7 copy-start.5
  137.9 0.7 copy-start.4
  137.9 1.1 copy-start.1
  144.8 4.3 %copy-start.6 = (f32[20]{0:T(128)S(1)}, f32[20]{0:T(128)}, u32[]{:S(2)}) copy-start(f32[20]{0:T(128)} %param.14) | copy-start | bytes 244
Sparse Core Ops, SparseCore 0:
  22.5 55.2 all-gather.7
  79.3 53.4 all-gather.5
  149.2 22.8 reduce-scatter.1
